TPU v7x, 128 devices: a whole 4x4x4 slice. The times are simulated.
128 devices in a mesh: fsdp: 16 (over z, x_lo, core), cols: 8 (over y, x_hi).
Axes of the slice: x: 4 (x_hi: 2, x_lo: 2; x = x_hi * 2 + x_lo), y: 4, z: 4, core: 2. Of those that a mesh axis runs over, the one named last changes fastest.
Arguments:
- weight_query: bfloat16 [5120, 5120], P('fsdp', 'cols'), may hold values from -0.078125 to 0.078125
- low_query: bfloat16 [5120, 32], P('fsdp'), may hold values from -0.078125 to 0.078125
- high_query: bfloat16 [32, 5120], P(None, 'cols'), may hold values from -1 to 1
- weight_key: bfloat16 [5120, 5120], P('fsdp', 'cols'), may hold values from -0.078125 to 0.078125
- low_key: bfloat16 [5120, 32], P('fsdp'), may hold values from -0.078125 to 0.078125
- high_key: bfloat16 [32, 5120], P(None, 'cols'), may hold values from -1 to 1
- weight_value: bfloat16 [5120, 5120], P('fsdp', 'cols'), may hold values from -0.078125 to 0.078125
- low_value: bfloat16 [5120, 32], P('fsdp'), may hold values from -0.078125 to 0.078125
- high_value: bfloat16 [32, 5120], P(None, 'cols'), may hold values from -1 to 1
- weight_mixed: bfloat16 [5120, 5120], P('cols', 'fsdp'), may hold values from -0.078125 to 0.078125
- low_mixed: bfloat16 [5120, 32], P('cols'), may hold values from -0.078125 to 0.078125
- high_mixed: bfloat16 [32, 5120], P(None, 'fsdp'), may hold values from -1 to 1
- norm_train: float32 [5120], P(('fsdp', 'cols')), may hold values from 0.25 to 1.75
- norm_step: float32 [5120], P(('fsdp', 'cols')), may hold values from -0.3 to 0.3
Outputs:
- ready_query: bfloat16 [5120, 5120], P(None, 'cols')
- ready_key: bfloat16 [5120, 5120], P(None, 'cols')
- ready_value: bfloat16 [5120, 5120], P(None, 'cols')
- ready_mixed: bfloat16 [5120, 5120], P('cols')
- serve_norm: bfloat16 [5120], replicated
All inputs are finite; a program needn't handle non-finite values.
Results may differ from a plain program's by a relative error of at most 0.001.
Values may be sent and summed in bfloat16 or wider, within the bound.
No kernel may reach another device: no remote copies, remote signals or barrier semaphores. Data moves between devices by JAX's collectives and lax.ppermute only.
A program may use at most 192 MiB of HBM per device.

v0:
```python
import jax
import jax.numpy as jnp
from jax import lax
from jax.sharding import PartitionSpec as P

mix_rate = 2.0


def rows_first(arrays, axis, dims):
    turned = [jnp.moveaxis(a, dim, 0) for a, dim in zip(arrays, dims)]
    widths = [t[0].size for t in turned]
    both = jnp.concatenate([t.reshape(-1, w) for t, w in zip(turned, widths)], axis=1)
    result = lax.all_gather(both, axis, axis=0, tiled=True)
    blocks = jnp.split(result, [sum(widths[:k]) for k in range(1, len(widths))], axis=1)
    return tuple(
        (
            jnp.moveaxis(b.reshape(-1, *t.shape[1:]), 0, dim)
            for b, t, dim in zip(blocks, turned, dims)
        )
    )


def per_device(
    weight_query,
    low_query,
    high_query,
    weight_key,
    low_key,
    high_key,
    weight_value,
    low_value,
    high_value,
    weight_mixed,
    low_mixed,
    high_mixed,
    norm_train,
    norm_step,
):
    latest_query = weight_query.astype(jnp.float32) + mix_rate * jnp.dot(
        low_query, high_query, preferred_element_type=jnp.float32
    )
    latest_key = weight_key.astype(jnp.float32) + mix_rate * jnp.dot(
        low_key, high_key, preferred_element_type=jnp.float32
    )
    latest_value = weight_value.astype(jnp.float32) + mix_rate * jnp.dot(
        low_value, high_value, preferred_element_type=jnp.float32
    )
    latest_mixed = weight_mixed.astype(jnp.float32) + mix_rate * jnp.dot(
        low_mixed, high_mixed, preferred_element_type=jnp.float32
    )
    narrow_query, narrow_key, narrow_value, narrow_mixed = (
        latest_query.astype(jnp.bfloat16),
        latest_key.astype(jnp.bfloat16),
        latest_value.astype(jnp.bfloat16),
        latest_mixed.astype(jnp.bfloat16),
    )
    ready_query, ready_key, ready_value, ready_mixed = rows_first(
        (narrow_query, narrow_key, narrow_value, narrow_mixed), "fsdp", (0, 0, 0, 1)
    )
    serve_norm = lax.all_gather(
        (norm_train + norm_step).astype(jnp.bfloat16), ("fsdp", "cols"), axis=0, tiled=True
    )
    return (ready_query, ready_key, ready_value, ready_mixed, serve_norm)


def solution(mesh):
    in_specs = (
        P("fsdp", "cols"),
        P("fsdp", None),
        P(None, "cols"),
        P("fsdp", "cols"),
        P("fsdp", None),
        P(None, "cols"),
        P("fsdp", "cols"),
        P("fsdp", None),
        P(None, "cols"),
        P("cols", "fsdp"),
        P("cols", None),
        P(None, "fsdp"),
        P(("fsdp", "cols")),
        P(("fsdp", "cols")),
    )
    out_specs = (P(None, "cols"), P(None, "cols"), P(None, "cols"), P("cols", None), P())
    return jax.shard_map(
        per_device, mesh=mesh, in_specs=in_specs, out_specs=out_specs, check_vma=False
    )
```

profile of v0, /device:TPU:1, one launch (start us, length us, event | category | flops | bytes accessed | tf_op | source)
XLA Modules:
  0.0 190.2 jit_solution(9804116227767435953)
XLA Ops:
  7.2 0.0 copy-start
  7.2 0.0 all-gather.2.cloned.1.call-start
  7.2 0.7 copy-done
  8.0 1.3 fusion.4
  9.3 1.3 fusion.5
  10.6 0.0 copy-start.1
  10.6 0.0 copy-start.2
  10.6 1.3 fusion.6
  12.0 1.4 fusion.8
  13.4 1.3 pad_maximum_fusion
  14.7 0.0 all-gather.2.cloned.1.call-update
  14.7 0.0 copy-done.1
  14.7 0.0 copy-done.2
  14.7 0.2 dynamic-update-slice
  15.0 68.9 %all-reduce = bf16[5120]{0:T(1024)(128)(2,1)} all-reduce(bf16[5120]{0:T(1024)(128)(2,1)S(1)} %dynamic-update-slice), channel_id=1, replica_groups=mesh['fsdp'=16,'cols'=8] {'fsdp','cols'}, use_global_device_ids=true, to_apply=%add | all-reduce | flops 5120 | bytes 20480
  83.9 71.9 %all-gather.2.cloned.1.call-done = bf16[5120,2560]{1,0:T(8,128)(2,1)} async-done(((bf16[320,2560]{1,0:T(8,128)(2,1)}), bf16[5120,2560]{1,0:T(8,128)(2,1)}) %all-gather.2.cloned.1.call-update) | async-done | bytes 26214416 | tf_op jit(solution)/shard_map/all_gather | solution.py:13
  155.7 18.1 %slice_bitcast_fusion = (bf16[640,5120]{0,1:T(8,128)(2,1)}, bf16[5120,640]{1,0:T(8,128)(2,1)}, bf16[5120,640]{1,0:T(8,128)(2,1)}, bf16[5120,640]{1,0:T(8,128)(2,1)}) fusion(bf16[5120,2560]{1,0:T(8,128)(2,1)} %all-gather.2.cloned.1.call-done), kind=kLoop, calls=%fused_computation | loop fusion | bytes 52428800 | tf_op jit(solution)/shard_map/transpose | solution.py:17
  173.8 9.5 %copy.19 = bf16[640,5120]{1,0:T(8,128)(2,1)} copy(bf16[640,5120]{0,1:T(8,128)(2,1)} %get-tuple-element.10) | data formatting | bytes 13107200
  (2 shorter events, 0.0 us)
Async XLA Ops:
  7.2 0.8 copy-start
  7.2 148.5 %all-gather.2.cloned.1.call-start = ((), (), s32[]{:S(2)}) async-start(), calls=%async_computation | async-start | bytes 27852800 | tf_op jit(solution)/shard_map/all_gather | solution.py:13
  10.6 4.1 %copy-start.1 = (f32[40]{0:T(128)S(1)}, f32[40]{0:T(128)}, u32[]{:S(2)}) copy-start(f32[40]{0:T(128)} %param.26) | copy-start | bytes 484
  10.6 4.1 %copy-start.2 = (f32[40]{0:T(128)S(1)}, f32[40]{0:T(128)}, u32[]{:S(2)}) copy-start(f32[40]{0:T(128)} %param.27) | copy-start | bytes 484
Sparse Core Ops, SparseCore 0:
  14.8 140.8 all-gather.1
where the time goes:
time: 191 us; the launch traced here: 190 us
  waiting for transfers between devices  71.9 us (38%)
  blocking collectives  68.9 us (36%)
  local copies, waits for them, and re-layouts  28.6 us (15%)
  between operations  14.1 us (7%)
  matrix products  5.36 us (3%)
    all_gather x1, waiting for transfers between devices, rows_first(): result = lax.all_gather(both, axis, axis=0, tiled=True)  71.9 us
    unnamed x1, blocking collectives  68.9 us
    transpose x1, local copies, waits for them, and re-layouts, rows_first(): jnp.moveaxis(b.reshape(-1, *t.shape[1:]), 0, dim)  18.1 us
    unnamed x9, local copies, waits for them, and re-layouts  10.5 us
  transfers between devices with their start and end apart: 1, of which 1 were waited for; matrix products, arithmetic and copies ran while one was open for 0% of the time, Pallas kernels for 0%

commit v1 on v0

--- a/solution.py
+++ b/solution.py
@@ -10,7 +10,8 @@
     turned = [jnp.moveaxis(a, dim, 0) for a, dim in zip(arrays, dims)]
     widths = [t[0].size for t in turned]
     both = jnp.concatenate([t.reshape(-1, w) for t, w in zip(turned, widths)], axis=1)
-    result = lax.all_gather(both, axis, axis=0, tiled=True)
+    repeated = jnp.stack([both] * lax.axis_size(axis))
+    result = jnp.concatenate(lax.all_to_all(repeated, axis, 0, 0), axis=0)
     blocks = jnp.split(result, [sum(widths[:k]) for k in range(1, len(widths))], axis=1)
     return tuple(
         (

time: 191 us -> 393 us (2.06)
  blocking collectives: 68.9 us -> 341 us
  waiting for transfers between devices: 71.9 us -> 0.01 us
  between operations: 14.1 us -> 0.7 us
  local copies, waits for them, and re-layouts: 28.6 us -> 37.6 us
  starting transfers between devices: 0.04 us -> 7.88 us
    unnamed x1, blocking collectives: 68.9 us -> 341 us
    all_gather x1 -> x0, waiting for transfers between devices: 71.9 us -> none  [rows_first(): result = lax.all_gather(both, axis, axis=0, tiled=True)]
    another operation x0 -> x1, local copies, waits for them, and re-layouts: none -> 8.9 us  [rows_first(): repeated = jnp.stack([both] * lax.axis_size(axis))]
    all_to_all x0 -> x1, starting transfers between devices: none -> 7.88 us  [rows_first(): result = jnp.concatenate(lax.all_to_all(repeated, axis, 0, 0), axis=0)]
    unnamed x9 -> x11, local copies, waits for them, and re-layouts: 10.5 us -> 10.6 us
  transfers between devices with their start and end apart: 1 -> 1, of which waited for: 1 -> 0; matrix products, arithmetic and copies ran while one was open for 0% -> 0% of each run, Pallas kernels for 0% -> 0%
where the time goes in v1:
time: 393 us
  blocking collectives  341 us (87%)
  local copies, waits for them, and re-layouts  37.6 us (10%)
  starting transfers between devices  7.88 us (2%)
  matrix products  5.36 us (1%)
    unnamed x1, blocking collectives  341 us
    transpose x1, local copies, waits for them, and re-layouts, rows_first(): jnp.moveaxis(b.reshape(-1, *t.shape[1:]), 0, dim)  18.1 us
    unnamed x11, local copies, waits for them, and re-layouts  10.6 us
    another operation x1, local copies, waits for them, and re-layouts, rows_first(): repeated = jnp.stack([both] * lax.axis_size(axis))  8.9 us
    all_to_all x1, starting transfers between devices, rows_first(): result = jnp.concatenate(lax.all_to_all(repeated, axis, 0, 0), axis=0)  7.88 us
  transfers between devices with their start and end apart: 1, of which 0 were waited for; matrix products, arithmetic and copies ran while one was open for 0% of the time, Pallas kernels for 0%

profile of v1, /device:TPU:1, one launch (start us, length us, event | category | flops | bytes accessed | tf_op | source)
XLA Modules:
  0.0 392.7 jit_solution(11650202632882592164)
XLA Ops:
  0.6 0.0 copy-start
  0.6 0.8 copy-done
  1.4 1.3 fusion.4
  2.7 1.3 fusion.5
  4.1 1.3 fusion.6
  5.4 1.4 fusion.8
  6.8 0.1 pad_maximum_fusion
  6.9 8.9 %stack.2 = bf16[16,320,2560]{2,1,0:T(8,128)(2,1)} broadcast(bf16[320,2560]{1,0:T(8,128)(2,1)S(1)} %pad_maximum_fusion), dimensions={1,2} | broadcast | bytes 27852800 | tf_op jit(solution)/shard_map/stack | solution.py:13
  15.8 0.0 copy-start.2
  15.8 0.0 copy-start.3
  15.8 7.9 %all-to-all-start = ((bf16[16,320,2560]{2,1,0:T(8,128)(2,1)}), bf16[16,320,2560]{2,1,0:T(8,128)(2,1)}, u32[]{:S(2)}, u32[]{:S(2)}) async-start(bf16[16,320,2560]{2,1,0:T(8,128)(2,1)} %stack.2), calls=%async_computation | async-start | bytes 52428800 | tf_op jit(solution)/shard_map/all_to_all | solution.py:14
  23.7 0.0 copy-done.2
  23.7 0.0 copy-done.3
  23.8 0.2 dynamic-update-slice
  24.0 341.1 %all-reduce = bf16[5120]{0:T(1024)(128)(2,1)} all-reduce(bf16[5120]{0:T(1024)(128)(2,1)S(1)} %dynamic-update-slice), channel_id=1, replica_groups=mesh['fsdp'=16,'cols'=8] {'fsdp','cols'}, use_global_device_ids=true, to_apply=%add | all-reduce | flops 5120 | bytes 20480
  365.1 0.0 all-to-all-done
  365.1 18.1 %slice_bitcast_fusion = (bf16[640,5120]{0,1:T(8,128)(2,1)}, bf16[5120,640]{1,0:T(8,128)(2,1)}, bf16[5120,640]{1,0:T(8,128)(2,1)}, bf16[5120,640]{1,0:T(8,128)(2,1)}) fusion(bf16[5120,2560]{1,0:T(8,128)(2,1)} %bitcast.1), kind=kLoop, calls=%fused_computation | loop fusion | bytes 52428800 | tf_op jit(solution)/shard_map/transpose | solution.py:18
  383.2 0.0 copy-start.1
  383.2 9.5 %copy.23 = bf16[640,5120]{1,0:T(8,128)(2,1)} copy(bf16[640,5120]{0,1:T(8,128)(2,1)} %get-tuple-element.15) | data formatting | bytes 13107200
  392.7 0.0 copy-done.1
  (2 shorter events, 0.0 us)
Async XLA Ops:
  0.6 0.8 copy-start
  15.8 7.9 %copy-start.2 = (f32[40]{0:T(128)S(1)}, f32[40]{0:T(128)}, u32[]{:S(2)}) copy-start(f32[40]{0:T(128)} %param.26) | copy-start | bytes 484
  15.8 7.9 %copy-start.3 = (f32[40]{0:T(128)S(1)}, f32[40]{0:T(128)}, u32[]{:S(2)}) copy-start(f32[40]{0:T(128)} %param.27) | copy-start | bytes 484
  15.8 349.3 %all-to-all-start = ((bf16[16,320,2560]{2,1,0:T(8,128)(2,1)}), bf16[16,320,2560]{2,1,0:T(8,128)(2,1)}, u32[]{:S(2)}, u32[]{:S(2)}) async-start(bf16[16,320,2560]{2,1,0:T(8,128)(2,1)} %stack.2), calls=%async_computation | async-start | bytes 52428800 | tf_op jit(solution)/shard_map/all_to_all | solution.py:14
  383.2 9.5 %copy-start.1 = (bf16[32,640]{1,0:T(8,128)(2,1)S(1)}, bf16[32,640]{1,0:T(8,128)(2,1)}, u32[]{:S(2)}) copy-start(bf16[32,640]{1,0:T(8,128)(2,1)} %param.16) | copy-start | bytes 122884
